TPU v7x, 32 devices: a whole 2x2x4 slice. The times are simulated.
32 devices in a mesh: replica: 4 (over y, x), fsdp: 8 (over z, core).
Axes of the slice: x: 2, y: 2, z: 4, core: 2. Of those that a mesh axis runs over, the one named last changes fastest.
Arguments:
- codes: int32 [4, 8192, 4096], P('replica', None, 'fsdp'), may hold values from -127 to 127
- scales: float32 [4, 32, 8192], P('replica', 'fsdp'), may hold values from 0.002 to 0.03
- master: float32 [8192, 4096], P(('replica', 'fsdp')), may hold values from -6 to 6
- momentum: float32 [8192, 4096], P(('replica', 'fsdp')), may hold values from -6 to 6
Outputs:
- new_master: float32 [8192, 4096], P(('replica', 'fsdp'))
- new_momentum: float32 [8192, 4096], P(('replica', 'fsdp'))
- weights: bfloat16 [8192, 4096], P(None, 'fsdp')
All inputs are finite; a program needn't handle non-finite values.
Results may differ from a plain program's by a relative error of at most 0.0075.
Values may be sent and summed in bfloat16 or wider, within the bound.
A program may use at most 128 MiB of HBM per device.

v0:
```python
import jax
import jax.numpy as jnp
from jax import lax
from jax.sharding import PartitionSpec as P

outer_rate = 0.7
momentum_factor = 0.9


def dequantize(codes, scales):
    block_count = scales.shape[1]
    total_rows = codes.shape[1]
    width = codes.shape[2]
    scaled = codes[0].astype(jnp.float32).reshape(total_rows, block_count, width // block_count)
    return (scaled * jnp.transpose(scales[0])[:, :, None]).reshape(total_rows, width)


def outer_update(summed, master, momentum, replica_count):
    mean_delta = summed / replica_count
    new_momentum = momentum_factor * momentum + mean_delta
    new_master = master - outer_rate * (mean_delta + momentum_factor * new_momentum)
    return (new_master, new_momentum)


def local(codes, scales, master, momentum):
    replica_count = lax.axis_size("replica")
    delta_local = dequantize(codes, scales)
    partial_sum = lax.psum_scatter(
        delta_local.astype(jnp.bfloat16), "replica", scatter_dimension=0, tiled=True
    ).astype(jnp.float32)
    summed = lax.all_to_all(
        partial_sum.astype(jnp.bfloat16), "fsdp", split_axis=0, concat_axis=1, tiled=True
    ).astype(partial_sum.dtype)
    new_master, new_momentum = outer_update(summed, master, momentum, replica_count)
    rounded = new_master.astype(jnp.bfloat16)
    columns = lax.all_to_all(rounded, "fsdp", split_axis=1, concat_axis=0, tiled=True)
    weights = lax.all_gather(columns, "replica", axis=0, tiled=True)
    return (new_master, new_momentum, weights)


def solution(mesh):
    return jax.shard_map(
        local,
        mesh=mesh,
        in_specs=(
            P("replica", None, "fsdp"),
            P("replica", "fsdp", None),
            P(("replica", "fsdp"), None),
            P(("replica", "fsdp"), None),
        ),
        out_specs=(P(("replica", "fsdp"), None), P(("replica", "fsdp"), None), P(None, "fsdp")),
        check_vma=False,
    )
```

profile of v0, /device:TPU:0, one launch (start us, length us, event | category | flops | bytes accessed | tf_op | source)
XLA Modules:
  0.0 348.3 jit_solution(17330387453719186282)
XLA Ops:
  7.2 0.0 reduce-scatter.2.cloned.1.call-start
  7.2 3.5 %copy.12 = f32[8192,4]{1,0:T(8,128)} copy(f32[8192,4]{0,1:T(4,128)} %bitcast.31) | data formatting | bytes 262144 | tf_op jit(solution)/shard_map/transpose | solution.py:15
  10.7 15.9 %mul.23 = f32[8192,4,128]{2,1,0:T(4,128)S(1)} broadcast(f32[8192,4]{1,0:T(8,128)} %copy.12), dimensions={0,1} | broadcast | bytes 16908288 | tf_op jit(solution)/shard_map/mul | solution.py:15
  26.6 11.6 %fusion = bf16[8192,512]{1,0:T(8,128)(2,1)} fusion(f32[1024,8,4,128]{3,2,1,0:T(4,128)S(1)} %bitcast.26, s32[1,8192,512]{2,1,0:T(8,128)} %param.4), kind=kLoop, calls=%fused_computation.1 | loop fusion | flops 12582912 | bytes 41943040 | tf_op jit(solution)/shard_map/convert_element_type | solution.py:29
  38.2 0.0 reduce-scatter.2.cloned.1.call-update
  38.3 89.2 %reduce-scatter.2.cloned.1.call-done = bf16[2048,512]{1,0:T(8,128)(2,1)} async-done(((bf16[8192,512]{1,0:T(8,128)(2,1)}), bf16[2048,512]{1,0:T(8,128)(2,1)}) %reduce-scatter.2.cloned.1.call-update) | async-done | bytes 2097168 | tf_op jit(solution)/shard_map/reduce_scatter | solution.py:28
  127.5 4.6 %all-to-all-start = ((bf16[8,256,512]{2,1,0:T(8,128)(2,1)}), bf16[8,256,512]{2,1,0:T(8,128)(2,1)S(1)}, u32[]{:S(2)}, u32[]{:S(2)}) async-start(bf16[8,256,512]{2,1,0:T(8,128)(2,1)} %bitcast.30), calls=%async_computation.1 | async-start | bytes 4194304 | tf_op jit(solution)/shard_map/all_to_all | solution.py:31
  132.1 0.0 all-gather.2.cloned.1.call-start
  132.1 5.6 %copy.14 = f32[256,4096]{0,1:T(8,128)} copy(f32[256,4096]{1,0:T(8,128)} %param.7) | data formatting | bytes 8388608 | tf_op args[3]
  137.7 5.6 %copy.15 = f32[256,4096]{0,1:T(8,128)} copy(f32[256,4096]{1,0:T(8,128)} %param.6) | data formatting | bytes 8388608 | tf_op args[2]
  143.3 37.8 %all-to-all-done = bf16[8,256,512]{2,1,0:T(8,128)(2,1)S(1)} async-done(((bf16[8,256,512]{2,1,0:T(8,128)(2,1)}), bf16[8,256,512]{2,1,0:T(8,128)(2,1)S(1)}, u32[]{:S(2)}, u32[]{:S(2)}) %all-to-all-start) | async-done | bytes 2097184 | tf_op jit(solution)/shard_map/all_to_all | solution.py:31
  181.1 2.4 copy.13
  183.5 0.0 copy-start
  183.5 2.1 convert_multiply_fusion
  185.6 0.7 copy-done
  186.3 7.3 %fusion.3 = (bf16[256,4096]{0,1:T(8,128)(2,1)}, f32[256,4096]{0,1:T(8,128)}, f32[256,4096]{0,1:T(8,128)}) fusion(f32[256,4096]{0,1:T(8,128)} %copy.15, f32[256,4096]{0,1:T(8,128)S(1)} %copy-done, f32[8,256,512]{1,2,0:T(8,128)S(1)} %convert_multiply_fusion), kind=kLoop, calls=%fused_computation.7 | loop fusion | flops 7340032 | bytes 23068672 | tf_op jit(solution)/shard_map/convert_element_type | solution.py:35
  193.5 52.5 %all_to_all.32 = bf16[256,8,512]{0,2,1:T(8,128)(2,1)S(1)} all-to-all(bf16[256,8,512]{0,2,1:T(8,128)(2,1)} %bitcast.29), channel_id=1, replica_groups=mesh['replica'=4,'fsdp'=8] {'fsdp'}, dimensions={1} | all-to-all | bytes 4194304 | tf_op jit(solution)/shard_map/all_to_all | solution.py:36
  246.1 2.4 copy.16
  248.5 0.0 all-gather.2.cloned.1.call-update
  248.5 5.6 %copy.17 = f32[256,4096]{1,0:T(8,128)} copy(f32[256,4096]{0,1:T(8,128)} %get-tuple-element.7) | data formatting | bytes 8388608
  254.1 6.0 %copy.18 = f32[256,4096]{1,0:T(8,128)} copy(f32[256,4096]{0,1:T(8,128)} %get-tuple-element.8) | data formatting | bytes 8388608
  260.1 74.0 %all-gather.2.cloned.1.call-done = bf16[8192,512]{1,0:T(8,128)(2,1)} async-done(((bf16[2048,512]{1,0:T(8,128)(2,1)}), bf16[8192,512]{1,0:T(8,128)(2,1)}) %all-gather.2.cloned.1.call-update) | async-done | bytes 8388624 | tf_op jit(solution)/shard_map/all_gather | solution.py:37
  334.1 7.3 %copy.22 = bf16[8192,512]{1,0:T(8,128)(2,1)} copy(bf16[8192,512]{1,0:T(8,128)(2,1)} %all-gather.2.cloned.1.call-done) | data formatting | bytes 16777216
Async XLA Ops:
  7.2 120.3 %reduce-scatter.2.cloned.1.call-start = ((), (), s32[]{:S(2)}) async-start(), calls=%async_computation.3 | async-start | bytes 10485760 | tf_op jit(solution)/shard_map/reduce_scatter | solution.py:28
  127.5 53.7 %all-to-all-start = ((bf16[8,256,512]{2,1,0:T(8,128)(2,1)}), bf16[8,256,512]{2,1,0:T(8,128)(2,1)S(1)}, u32[]{:S(2)}, u32[]{:S(2)}) async-start(bf16[8,256,512]{2,1,0:T(8,128)(2,1)} %bitcast.30), calls=%async_computation.1 | async-start | bytes 4194304 | tf_op jit(solution)/shard_map/all_to_all | solution.py:31
  132.1 202.0 %all-gather.2.cloned.1.call-start = ((), (), s32[]{:S(2)}) async-start(), calls=%async_computation.4 | async-start | bytes 10485760 | tf_op jit(solution)/shard_map/all_gather | solution.py:37
  183.5 2.8 copy-start
Sparse Core Ops, SparseCore 0:
  38.4 89.0 reduce-scatter.1
  248.6 85.4 all-gather.1
where the time goes:
time: 349 us; the launch traced here: 348 us
  waiting for transfers between devices  201 us (58%)
  local copies, waits for them, and re-layouts  55 us (16%)
  blocking collectives  52.5 us (15%)
  other arithmetic  21 us (6%)
  between operations  14.1 us (4%)
  starting transfers between devices  4.69 us (1%)
    reduce_scatter x1, waiting for transfers between devices, local(): lax.psum_scatter(delta_local.astype(jnp.bfloat16), 'replica', scatter_dim...  89.2 us
    all_gather x1, waiting for transfers between devices, local(): weights = lax.all_gather(columns, 'replica', axis=0, tiled=True)  74 us
    all_to_all x1, blocking collectives, local(): lax.all_to_all(rounded, 'fsdp', split_axis=1, concat_axis=0, tiled=True)  52.5 us
    all_to_all x1, waiting for transfers between devices, local(): lax.all_to_all(partial_sum.astype(jnp.bfloat16), 'fsdp', split_axis=0, co...  37.8 us
    unnamed x7, local copies, waits for them, and re-layouts  30.8 us
    mul x1, local copies, waits for them, and re-layouts, dequantize(): scaled * jnp.transpose(scales[0])[:, :, None]  15.9 us
    convert_element_type x1, other arithmetic, local(): delta_local.astype(jnp.bfloat16)  11.6 us
    convert_element_type x1, other arithmetic, local(): rounded = new_master.astype(jnp.bfloat16)  7.26 us
  transfers between devices with their start and end apart: 3, of which 3 were waited for; matrix products, arithmetic and copies ran while one was open for 7% of the time, Pallas kernels for 0%

commit v1 on v0

--- a/solution.py
+++ b/solution.py
@@ -28,8 +28,14 @@
     partial_sum = lax.psum_scatter(
         delta_local.astype(jnp.bfloat16), "replica", scatter_dimension=0, tiled=True
     ).astype(jnp.float32)
-    summed = lax.all_to_all(
-        partial_sum.astype(jnp.bfloat16), "fsdp", split_axis=0, concat_axis=1, tiled=True
+    summed = jnp.concatenate(
+        lax.all_to_all(
+            jnp.stack(jnp.split(partial_sum.astype(jnp.bfloat16), lax.axis_size("fsdp"), axis=0)),
+            "fsdp",
+            0,
+            0,
+        ),
+        axis=1,
     ).astype(partial_sum.dtype)
     new_master, new_momentum = outer_update(summed, master, momentum, replica_count)
     rounded = new_master.astype(jnp.bfloat16)

time: 349 us -> 351 us (level)
  blocking collectives: 52.5 us -> 106 us
  waiting for transfers between devices: 201 us -> 175 us
  local copies, waits for them, and re-layouts: 55 us -> 35.1 us
  starting transfers between devices: 4.69 us -> 0.08 us
    all_to_all x0 -> x1, blocking collectives: none -> 53.4 us  [local(): lax.all_to_all(jnp.stack(jnp.split(partial_sum.astype(jnp.bfloat16), lax....]
    all_to_all x1 -> x0, waiting for transfers between devices: 37.8 us -> none  [local(): lax.all_to_all(partial_sum.astype(jnp.bfloat16), 'fsdp', split_axis=0, co...]
    unnamed x7 -> x8, local copies, waits for them, and re-layouts: 30.8 us -> 14.1 us
    all_gather x1, waiting for transfers between devices: 74 us -> 85.6 us  [local(): weights = lax.all_gather(columns, 'replica', axis=0, tiled=True)]
    all_to_all x1 -> x0, starting transfers between devices: 4.62 us -> none  [local(): lax.all_to_all(partial_sum.astype(jnp.bfloat16), 'fsdp', split_axis=0, co...]
  transfers between devices with their start and end apart: 3 -> 2, of which waited for: 3 -> 2; matrix products, arithmetic and copies ran while one was open for 7% -> 0% of each run, Pallas kernels for 0% -> 0%
where the time goes in v1:
time: 351 us
  waiting for transfers between devices  175 us (50%)
  blocking collectives  106 us (30%)
  local copies, waits for them, and re-layouts  35.1 us (10%)
  other arithmetic  21 us (6%)
  between operations  14.1 us (4%)
    reduce_scatter x1, waiting for transfers between devices, local(): lax.psum_scatter(delta_local.astype(jnp.bfloat16), 'replica', scatter_dim...  89.1 us
    all_gather x1, waiting for transfers between devices, local(): weights = lax.all_gather(columns, 'replica', axis=0, tiled=True)  85.6 us
    all_to_all x1, blocking collectives, local(): lax.all_to_all(jnp.stack(jnp.split(partial_sum.astype(jnp.bfloat16), lax....  53.4 us
    all_to_all x1, blocking collectives, local(): lax.all_to_all(rounded, 'fsdp', split_axis=1, concat_axis=0, tiled=True)  52.2 us
    mul x1, local copies, waits for them, and re-layouts, dequantize(): scaled * jnp.transpose(scales[0])[:, :, None]  15.9 us
    unnamed x8, local copies, waits for them, and re-layouts  14.1 us
    convert_element_type x1, other arithmetic, local(): delta_local.astype(jnp.bfloat16)  11.6 us
    convert_element_type x1, other arithmetic, local(): rounded = new_master.astype(jnp.bfloat16)  8.85 us
  transfers between devices with their start and end apart: 2, of which 2 were waited for; matrix products, arithmetic and copies ran while one was open for 0% of the time, Pallas kernels for 0%

profile of v1, /device:TPU:0, one launch (start us, length us, event | category | flops | bytes accessed | tf_op | source)
XLA Modules:
  0.0 350.7 jit_solution(15415753327921154262)
XLA Ops:
  7.2 0.0 reduce-scatter.2.cloned.1.call-start
  7.2 3.5 copy.7
  10.7 15.9 %mul.23 = f32[8192,4,128]{2,1,0:T(4,128)S(1)} broadcast(f32[8192,4]{1,0:T(8,128)} %copy.7), dimensions={0,1} | broadcast | bytes 16908288 | tf_op jit(solution)/shard_map/mul | solution.py:15
  26.6 11.6 %fusion = bf16[8192,512]{1,0:T(8,128)(2,1)} fusion(f32[1024,8,4,128]{3,2,1,0:T(4,128)S(1)} %bitcast.53, s32[1,8192,512]{2,1,0:T(8,128)} %param.4), kind=kLoop, calls=%fused_computation.1 | loop fusion | flops 12582912 | bytes 41943040 | tf_op jit(solution)/shard_map/convert_element_type | solution.py:29
  38.2 0.0 reduce-scatter.2.cloned.1.call-update
  38.3 0.0 all-gather.2.cloned.1.call-start
  38.3 89.1 %reduce-scatter.2.cloned.1.call-done = bf16[2048,512]{1,0:T(8,128)(2,1)} async-done(((bf16[8192,512]{1,0:T(8,128)(2,1)}), bf16[2048,512]{1,0:T(8,128)(2,1)}) %reduce-scatter.2.cloned.1.call-update) | async-done | bytes 2097168 | tf_op jit(solution)/shard_map/reduce_scatter | solution.py:28
  127.5 1.0 fusion.8
  128.4 1.0 fusion.7
  129.4 1.0 fusion.6
  130.4 1.0 fusion.5
  131.3 1.0 fusion.4
  132.3 1.0 fusion.3
  133.3 1.0 fusion.2
  134.3 1.0 fusion.1
  135.2 53.4 %all_to_all.24 = bf16[8,256,512]{2,1,0:T(8,128)(2,1)S(1)} all-to-all(bf16[8,256,512]{2,1,0:T(8,128)(2,1)S(1)} %fusion.1), channel_id=1, replica_groups=mesh['replica'=4,'fsdp'=8] {'fsdp'}, dimensions={0} | all-to-all | bytes 4194304 | tf_op jit(solution)/shard_map/all_to_all | solution.py:32
  188.7 0.6 multiply_bitcast_fusion
  189.3 0.5 copy.11
  189.7 8.8 %fusion.9 = (bf16[256,4096]{1,0:T(8,128)(2,1)S(1)}, f32[256,4096]{1,0:T(8,128)}, f32[256,4096]{1,0:T(8,128)}) fusion(f32[256,4096]{1,0:T(8,128)} %param.6, f32[256,4096]{1,0:T(8,128)S(1)} %bitcast.54, f32[256,4096]{1,0:T(8,128)} %param.7), kind=kLoop, calls=%fused_computation.22 | loop fusion | flops 7340032 | bytes 23068672 | tf_op jit(solution)/shard_map/convert_element_type | solution.py:41
  198.6 0.2 copy.15
  198.8 52.2 %all_to_all.25 = bf16[256,8,512]{2,0,1:T(8,128)(2,1)} all-to-all(bf16[256,8,512]{2,0,1:T(8,128)(2,1)S(1)} %bitcast.56), channel_id=1, replica_groups=mesh['replica'=4,'fsdp'=8] {'fsdp'}, dimensions={1} | all-to-all | bytes 4194304 | tf_op jit(solution)/shard_map/all_to_all | solution.py:42
  251.0 0.0 all-gather.2.cloned.1.call-update
  251.0 85.6 %all-gather.2.cloned.1.call-done = bf16[8192,512]{1,0:T(8,128)(2,1)} async-done(((bf16[2048,512]{1,0:T(8,128)(2,1)}), bf16[8192,512]{1,0:T(8,128)(2,1)}) %all-gather.2.cloned.1.call-update) | async-done | bytes 8388624 | tf_op jit(solution)/shard_map/all_gather | solution.py:43
  336.6 7.3 %copy.24 = bf16[8192,512]{1,0:T(8,128)(2,1)} copy(bf16[8192,512]{1,0:T(8,128)(2,1)} %all-gather.2.cloned.1.call-done) | data formatting | bytes 16777216
Async XLA Ops:
  7.2 120.3 %reduce-scatter.2.cloned.1.call-start = ((), (), s32[]{:S(2)}) async-start(), calls=%async_computation.3 | async-start | bytes 10485760 | tf_op jit(solution)/shard_map/reduce_scatter | solution.py:28
  38.3 298.3 %all-gather.2.cloned.1.call-start = ((), (), s32[]{:S(2)}) async-start(), calls=%async_computation.4 | async-start | bytes 10485760 | tf_op jit(solution)/shard_map/all_gather | solution.py:43
Sparse Core Ops, SparseCore 0:
  38.4 89.0 reduce-scatter.1
  251.1 85.4 all-gather.1
